TPU v7x, 32 devices: a whole 2x2x4 slice. The times are simulated.
32 devices in a mesh: role: 2 (over x), grp: 2 (over y), tp: 8 (over z, core).
Axes of the slice: x: 2, y: 2, z: 4, core: 2. Of those that a mesh axis runs over, the one named last changes fastest.
Arguments:
- queries: bfloat16 [2, 8, 8192], P(None, None, ('grp', 'tp')), may hold values from -130 to 130
- step_token_keys: bfloat16 [2, 8, 1024], replicated, may hold values from -6 to 6
- step_token_values: bfloat16 [2, 8, 1024], replicated, may hold values from -6 to 6
- stored_key_cache: bfloat16 [8, 512, 1024], P(None, ('grp', 'tp')), may hold values from -6 to 6
- stored_value_cache: bfloat16 [8, 512, 1024], P(None, ('grp', 'tp')), may hold values from -6 to 6
- lengths: int32 [8], replicated, may hold values from 2 to 512
- wo_sides: bfloat16 [2, 8192, 8192], P('role', ('grp', 'tp')), may hold values from -1 to 1
- gain_sides: float32 [2, 8192], P('role', ('grp', 'tp')), may hold values from 0.5 to 1.5
- head: bfloat16 [8192, 64128], P(None, ('grp', 'tp')), may hold values from -8 to 8
- resid: bfloat16 [2, 8, 8192], P(None, None, ('grp', 'tp')), may hold values from -90 to 90
- actions: int32 [2, 8], replicated, may hold values from 0 to 64127
Outputs:
- log_probs: float32 [2, 8], P('role')
- normed: bfloat16 [2, 8, 8192], P('role', None, ('grp', 'tp'))
All inputs are finite; a program needn't handle non-finite values.
Results may differ from a plain program's by a relative error of at most 0.017.
Values may be sent and summed in bfloat16 or wider, within the bound.
A program may use at most 128 MiB of HBM per device.

v0:
```python
import functools
import math

import jax
import jax.numpy as jnp
from jax import lax
from jax.experimental import pallas as pl
from jax.experimental.pallas import tpu as pltpu
from jax.sharding import PartitionSpec as P

D = 8192
QUERY_HEADS = 64
KEY_VALUE_HEADS = 8
HEAD_SIZE = 128
DECODE_STEPS = 2


def swap_sides(value):
    return lax.ppermute(value, "role", [(0, 1), (1, 0)])


def plain(
    queries,
    step_token_keys,
    step_token_values,
    stored_key_cache,
    stored_value_cache,
    lengths,
    wo_sides,
    gain_sides,
    head,
    resid,
    actions,
):
    both = ("grp", "tp")
    place = lax.axis_index(both)
    step = 1 - lax.axis_index("role")
    count_of_rows = lengths.shape[0]
    shard_length = stored_key_cache.shape[1]
    query_group_width = QUERY_HEADS // KEY_VALUE_HEADS
    logit_scale = 1.0 / math.sqrt(HEAD_SIZE)
    query_matrix = lax.all_gather(
        lax.dynamic_index_in_dim(queries, step, 0, keepdims=False), both, axis=1, tiled=True
    )
    positions = place * shard_length + jnp.arange(shard_length, dtype=jnp.int32)
    valid = positions[None, :] < lengths[:, None]
    masking = valid[:, None, None, :]
    cache_shape = (count_of_rows, shard_length, KEY_VALUE_HEADS, HEAD_SIZE)
    prior_keys = stored_key_cache.reshape(cache_shape)
    prior_values = stored_value_cache.reshape(cache_shape)
    step_shape = (DECODE_STEPS, count_of_rows, KEY_VALUE_HEADS, HEAD_SIZE)
    incoming_keys = step_token_keys.astype(jnp.float32).reshape(step_shape)
    incoming_values = step_token_values.astype(jnp.float32).reshape(step_shape)
    current_query = query_matrix.reshape(
        count_of_rows, KEY_VALUE_HEADS, query_group_width, HEAD_SIZE
    )
    scores = (
        jnp.einsum("rkgd,rskd->rkgs", current_query, prior_keys, preferred_element_type=jnp.float32)
        * logit_scale
    )
    scores = jnp.where(masking, scores, -1e30)
    fresh_live = jnp.arange(DECODE_STEPS, dtype=jnp.int32) <= step
    fresh_scores = (
        jnp.einsum("rkgd,trkd->rkgt", current_query.astype(jnp.float32), incoming_keys)
        * logit_scale
    )
    fresh_scores = jnp.where(fresh_live, fresh_scores, -1e30)
    fresh_highest = jnp.max(fresh_scores, axis=-1)
    overall = lax.pmax(jnp.maximum(jnp.max(scores, axis=-1), fresh_highest), both)
    cache_probs = jnp.exp(scores - overall[..., None]) * masking
    fresh_probs = jnp.exp(fresh_scores - overall[..., None]) * fresh_live
    fresh_probs = fresh_probs * (place == 0)
    totals = jnp.sum(cache_probs, axis=-1) + jnp.sum(fresh_probs, axis=-1)
    weighted = jnp.einsum(
        "rkgs,rskd->rkgd", cache_probs, prior_values.astype(jnp.float32)
    ) + jnp.einsum("rkgt,trkd->rkgd", fresh_probs, incoming_values)
    features = QUERY_HEADS * HEAD_SIZE
    mixed = lax.psum_scatter(
        weighted.reshape(count_of_rows, features), both, scatter_dimension=1, tiled=True
    )
    totals = lax.psum(totals.reshape(count_of_rows, QUERY_HEADS), both)
    feature_rows = wo_sides.shape[1]
    own_heads = (place * feature_rows + jnp.arange(feature_rows)) // HEAD_SIZE
    own_part = (mixed / jnp.take(totals, own_heads, axis=1)).astype(jnp.bfloat16)
    branch_out = lax.psum_scatter(
        jnp.dot(own_part, wo_sides[0], preferred_element_type=jnp.float32),
        both,
        scatter_dimension=1,
        tiled=True,
    )
    resid_now = lax.dynamic_index_in_dim(resid, step, 0, keepdims=False)
    state = resid_now.astype(jnp.float32) + branch_out
    square_sum = lax.psum(jnp.sum(state * state, axis=-1), both)
    normed_now = (
        state * lax.rsqrt(square_sum[:, None] / D + 1e-05) * gain_sides[0][None, :]
    ).astype(jnp.bfloat16)
    logits = jnp.dot(
        lax.all_gather(normed_now, both, axis=1, tiled=True),
        head,
        preferred_element_type=jnp.float32,
    )
    local_highest = jnp.max(logits, axis=-1)
    action_now = lax.dynamic_index_in_dim(actions, step, 0, keepdims=False)
    head_width = head.shape[1]
    vocab_ids = place * head_width + jnp.arange(head_width, dtype=jnp.int32)
    is_target = vocab_ids[None, :] == action_now[:, None]
    target = jnp.sum(jnp.where(is_target, logits, 0.0), axis=-1)
    exp_sum = jnp.sum(jnp.exp(logits - local_highest[:, None]), axis=-1)
    parts = lax.all_gather(jnp.stack([local_highest, exp_sum, target]), both)
    largest = jnp.max(parts[:, 0], axis=0)
    exp_sum = jnp.sum(parts[:, 1] * jnp.exp(parts[:, 0] - largest[None]), axis=0)
    prob_now = jnp.sum(parts[:, 2], axis=0) - largest - jnp.log(exp_sum)
    return (swap_sides(prob_now)[None], swap_sides(normed_now)[None])


LOW = -1e30
TILE = 512
MESH = pl.DeviceIdType.MESH


def fused_kernel(
    n,
    tp,
    queries,
    token_keys,
    token_values,
    keys_in,
    values_in,
    lengths,
    gain,
    resid,
    actions,
    wo,
    head,
    log_probs,
    normed,
    keys,
    values,
    wo_buf,
    head_buf,
    q_all,
    b_send,
    b_recv,
    c_send,
    c_recv,
    d_send,
    d_recv,
    x_send,
    x_recv,
    s_send,
    s_recv,
    x_rows,
    y_keep,
    y_send,
    y_recv,
    e_send,
    e_recv,
    kv_sems,
    wo_sem,
    head_sems,
    q_ss,
    q_rs,
    b_ss,
    b_rs,
    c_ss,
    c_rs,
    d_ss,
    d_rs,
    x_sem,
    s_ss,
    s_rs,
    y_ss,
    y_rs,
    e_ss,
    e_rs,
):
    role = lax.axis_index("role")
    me = lax.axis_index("grp") * tp + lax.axis_index("tp")
    step = 1 - role
    half = n // 2
    rows = lengths.shape[0]
    shard = keys.shape[1]
    width = resid.shape[2]
    own_heads = width // HEAD_SIZE
    group = QUERY_HEADS // KEY_VALUE_HEADS
    slots = rows * shard
    depth = head_buf.shape[1]
    vocab = head.shape[0]
    full = vocab // TILE
    tail = vocab - full * TILE
    tiles = y_keep.shape[0]
    scale = 1.0 / math.sqrt(HEAD_SIZE)
    f32 = jnp.float32
    bf16 = jnp.bfloat16

    def device(side, place):
        return (side, place // tp, place % tp)

    def remote(src, dst, ss, rs, side, place):
        return pltpu.make_async_remote_copy(
            src_ref=src,
            dst_ref=dst,
            send_sem=ss,
            recv_sem=rs,
            device_id=device(side, place),
            device_id_type=MESH,
        )

    key_copy = pltpu.make_async_copy(keys_in, keys, kv_sems.at[0])
    value_copy = pltpu.make_async_copy(values_in, values, kv_sems.at[1])
    key_copy.start()
    value_copy.start()
    wo_copy = pltpu.make_async_copy(wo.at[0], wo_buf, wo_sem)
    wo_copy.start()

    def head_copy(first, size, sem):
        return pltpu.make_async_copy(
            head.at[pl.ds(first, size), pl.ds(pl.multiple_of(role * depth, 128), depth)],
            head_buf.at[pl.ds(first, size), :],
            sem,
        )

    @pl.loop(0, full)
    def _(j):
        head_copy(pl.multiple_of(j * TILE, TILE), TILE, head_sems.at[j]).start()

    if tail:
        head_copy(full * TILE, tail, head_sems.at[full]).start()

    barrier = pltpu.get_barrier_semaphore()

    @pl.loop(1, 2 * n)
    def _(i):
        other = (role * n + me + i) % (2 * n)
        pl.semaphore_signal(
            barrier, inc=1, device_id=device(other // n, other % n), device_id_type=MESH
        )

    pl.semaphore_wait(barrier, 2 * n - 1)

    @pl.loop(1, n)
    def _(i):
        to = (me + i) % n
        remote(queries.at[step], q_all.at[me], q_ss.at[i], q_rs.at[me], role, to).start()

    q_all[me] = queries[step]

    row_ids = lax.broadcasted_iota(jnp.int32, (group * rows, slots), 0) % rows
    col_ids = lax.broadcasted_iota(jnp.int32, (group * rows, slots), 1)
    limit = jnp.zeros((group * rows, slots), jnp.int32)
    for b in range(rows):
        limit = jnp.where(row_ids == b, lengths[b], limit)
    place_ids = me * shard + col_ids % shard
    live = (col_ids // shard == row_ids) & (place_ids < limit)

    @pl.loop(1, n)
    def _(i):
        src = (me + i) % n
        remote(queries.at[step], q_all.at[src], q_ss.at[i], q_rs.at[src], role, me).wait_recv()

    key_copy.wait()
    value_copy.wait()

    lane = lax.broadcasted_iota(jnp.int32, (rows, HEAD_SIZE), 1)
    per_group = group // own_heads
    for k in range(KEY_VALUE_HEADS):
        lanes = slice(k * HEAD_SIZE, (k + 1) * HEAD_SIZE)
        query = jnp.concatenate(
            [
                q_all[
                    k * per_group + h // own_heads,
                    :,
                    (h % own_heads) * HEAD_SIZE : (h % own_heads + 1) * HEAD_SIZE,
                ].astype(f32)
                for h in range(group)
            ],
            axis=0,
        ).astype(bf16)
        key = keys[:, :, lanes].reshape(slots, HEAD_SIZE)
        value = values[:, :, lanes].reshape(slots, HEAD_SIZE)
        scores = (
            lax.dot_general(query, key, (((1,), (1,)), ((), ())), preferred_element_type=f32)
            * scale
        )
        scores = jnp.where(live, scores, LOW)
        top = jnp.max(scores, axis=1, keepdims=True).astype(bf16).astype(f32)
        probs = jnp.where(live, jnp.exp(scores - top), 0.0).astype(bf16)
        total = jnp.sum(probs.astype(f32), axis=1, keepdims=True)
        total_high = total.astype(bf16).astype(f32)
        total_low = total - total_high
        weighted = jnp.dot(probs, value, preferred_element_type=f32)
        for part in range(per_group):
            to = k * per_group + part
            stats = jnp.zeros((rows, HEAD_SIZE), f32)
            for j in range(own_heads):
                at = (part * own_heads + j) * rows
                stats = jnp.where(lane == j, top[at : at + rows], stats)
                stats = jnp.where(lane == own_heads + j, total_high[at : at + rows], stats)
                stats = jnp.where(lane == 2 * own_heads + j, total_low[at : at + rows], stats)
            first = part * own_heads * rows
            b_send[to] = jnp.concatenate(
                [weighted[first : first + own_heads * rows], stats, jnp.zeros_like(stats)], axis=0
            ).astype(bf16)

    @pl.loop(1, n)
    def _(i):
        to = (me + i) % n
        remote(b_send.at[to], b_recv.at[me], b_ss.at[i], b_rs.at[me], role, to).start()

    b_recv[me] = b_send[me]

    kv_lanes = pl.ds(pl.multiple_of((me // per_group) * HEAD_SIZE, HEAD_SIZE), HEAD_SIZE)
    own_query = queries[step].astype(f32)
    fresh = []
    fresh_values = []
    for u in range(DECODE_STEPS):
        fresh_key = token_keys[u, :, kv_lanes].astype(f32)
        fresh_values.append(token_values[u, :, kv_lanes].astype(f32))
        fresh.append(
            [
                jnp.where(
                    u <= step,
                    jnp.sum(
                        own_query[:, j * HEAD_SIZE : (j + 1) * HEAD_SIZE] * fresh_key,
                        axis=1,
                        keepdims=True,
                    )
                    * scale,
                    LOW,
                )
                for j in range(own_heads)
            ]
        )

    @pl.loop(1, n)
    def _(i):
        src = (me + i) % n
        remote(b_send.at[src], b_recv.at[src], b_ss.at[i], b_rs.at[src], role, me).wait_recv()

    stat_rows = slice(own_heads * rows, own_heads * rows + 16)
    stats = [b_recv[s, stat_rows, :].astype(f32)[:rows] for s in range(n)]
    top = functools.reduce(jnp.maximum, stats)
    tops = [
        functools.reduce(
            jnp.maximum, [fresh[u][j] for u in range(DECODE_STEPS)], top[:, j : j + 1]
        )
        for j in range(own_heads)
    ]
    numerator = [jnp.zeros((rows, HEAD_SIZE), f32) for _ in range(own_heads)]
    denominator = [jnp.zeros((rows, 1), f32) for _ in range(own_heads)]
    for j in range(own_heads):
        for u in range(DECODE_STEPS):
            weight = jnp.where(u <= step, jnp.exp(fresh[u][j] - tops[j]), 0.0)
            numerator[j] += weight * fresh_values[u]
            denominator[j] += weight
    for s in range(n):
        part = b_recv[s, : own_heads * rows, :].astype(f32)
        for j in range(own_heads):
            factor = jnp.exp(stats[s][:, j : j + 1] - tops[j])
            numerator[j] += factor * part[j * rows : (j + 1) * rows]
            at = own_heads + j
            denominator[j] += factor * (
                stats[s][:, at : at + 1] + stats[s][:, at + own_heads : at + own_heads + 1]
            )
    attended = jnp.concatenate(
        [numerator[j] / denominator[j] for j in range(own_heads)], axis=1
    ).astype(bf16)

    wo_copy.wait()

    def project(to):
        return jnp.dot(
            attended,
            wo_buf[:, pl.ds(pl.multiple_of(to * width, 128), width)],
            preferred_element_type=f32,
        )

    @pl.loop(1, n)
    def _(i):
        to = (me + i) % n
        c_send[to] = project(to).astype(bf16)
        remote(c_send.at[to], c_recv.at[me], c_ss.at[i], c_rs.at[me], role, to).start()

    c_recv[me] = jnp.zeros((rows, width), bf16)
    state = resid[step].astype(f32) + project(me)

    @pl.loop(1, n)
    def _(i):
        src = (me + i) % n
        remote(c_send.at[src], c_recv.at[src], c_ss.at[i], c_rs.at[src], role, me).wait_recv()

    for s in range(n):
        state += c_recv[s].astype(f32)

    x = state * gain[...]
    d_send[...] = x.astype(bf16)
    x_send[...] = x
    s_send[...] = jnp.broadcast_to(jnp.sum(state * state, axis=1, keepdims=True), (rows, HEAD_SIZE))
    target_role = me // half
    own_slot = role * half + me % half

    @pl.when(target_role != role)
    def _():
        remote(
            d_send, d_recv.at[own_slot], d_ss.at[0], d_rs.at[own_slot], target_role, me
        ).start()

    @pl.when(target_role == role)
    def _():
        d_recv[own_slot] = d_send[...]

    @pl.loop(1, n)
    def _(i):
        to = (me + i) % n
        remote(
            d_send, d_recv.at[own_slot], d_ss.at[i], d_rs.at[own_slot], target_role, to
        ).start()

    @pl.loop(0, n)
    def _(i):
        to = (me + i) % n
        remote(s_send, s_recv.at[me], s_ss.at[i], s_rs.at[me], 1 - role, to).start()

    remote(x_send, x_recv, x_sem.at[0], x_sem.at[1], 1 - role, me).start()

    @pl.loop(0, n)
    def _(slot):
        mine = (slot // half == role) & (role * half + slot % half == me)

        @pl.when(jnp.logical_not(mine))
        def _():
            remote(d_send, d_recv.at[slot], d_ss.at[0], d_rs.at[slot], role, me).wait_recv()

    for f in range(half):
        x_rows[:, f * width : (f + 1) * width] = jnp.concatenate(
            [d_recv[half + f].astype(f32), d_recv[f].astype(f32)], axis=0
        ).astype(bf16)

    def vocab_dot(block):
        return lax.dot_general(
            x_rows[...], block, (((1,), (1,)), ((), ())), preferred_element_type=f32
        )

    def y_copy(j):
        return remote(y_send.at[j], y_recv.at[j], y_ss.at[j], y_rs.at[j], 1 - role, me)

    @pl.loop(0, full)
    def _(j):
        first = pl.multiple_of(j * TILE, TILE)
        head_copy(first, TILE, head_sems.at[j]).wait()
        y = vocab_dot(head_buf[pl.ds(first, TILE), :])
        y_keep[j] = jnp.where(role == 0, y[:rows], y[rows:])
        y_send[j] = jnp.where(role == 0, y[rows:], y[:rows])
        y_copy(j).start()

    if tail:
        head_copy(full * TILE, tail, head_sems.at[full]).wait()
        y = vocab_dot(head_buf[full * TILE :, :])
        y_keep[full] = jnp.zeros((rows, TILE), f32)
        y_send[full] = jnp.zeros((rows, TILE), f32)
        y_keep[full, :, :tail] = jnp.where(role == 0, y[:rows], y[rows:])
        y_send[full, :, :tail] = jnp.where(role == 0, y[rows:], y[:rows])
        y_copy(full).start()

    @pl.loop(0, n)
    def _(s):
        remote(s_send, s_recv.at[s], s_ss.at[s], s_rs.at[s], role, me).wait_recv()

    square_sum = jnp.zeros((rows, HEAD_SIZE), f32)
    for s in range(n):
        square_sum += s_recv[s]
    inverse = lax.rsqrt(square_sum / (n * width) + 1e-05)[:, :1]
    remote(x_send, x_recv, x_sem.at[0], x_sem.at[1], role, me).wait_recv()
    normed[0] = (x_recv[...] * inverse).astype(bf16)

    action_rows = lax.broadcasted_iota(jnp.int32, (rows, 1), 0)
    action = jnp.zeros((rows, 1), jnp.int32)
    for b in range(rows):
        action = jnp.where(action_rows == b, actions[role, b], action)
    tile_ids = lax.broadcasted_iota(jnp.int32, (rows, TILE), 1)
    logits = []
    for j in range(tiles):
        y_copy(j).wait_recv()
        tile = (y_keep[j] + y_recv[j]) * inverse
        if j == full:
            tile = jnp.where(tile_ids < tail, tile, LOW)
        logits.append(tile)
    largest = jnp.max(functools.reduce(jnp.maximum, logits), axis=1, keepdims=True)
    exp_sum = jnp.zeros((rows, TILE), f32)
    target = jnp.zeros((rows, TILE), f32)
    for j in range(tiles):
        exp_sum += jnp.exp(logits[j] - largest)
        here = tile_ids + j * TILE == action - me * vocab
        if j == full:
            here = here & (tile_ids < tail)
        target += jnp.where(here, logits[j], 0.0)
    exp_sum = jnp.sum(exp_sum, axis=1, keepdims=True)
    target = jnp.sum(target, axis=1, keepdims=True)
    e_send[...] = jnp.where(lane == 0, largest, jnp.where(lane == 1, exp_sum, target))

    @pl.loop(1, n)
    def _(i):
        to = (me + i) % n
        remote(e_send, e_recv.at[me], e_ss.at[i], e_rs.at[me], role, to).start()

    e_recv[me] = e_send[...]

    @pl.loop(1, n)
    def _(i):
        src = (me + i) % n
        remote(e_send, e_recv.at[src], e_ss.at[i], e_rs.at[src], role, me).wait_recv()

    top = functools.reduce(jnp.maximum, [e_recv[s] for s in range(n)])[:, :1]
    exp_sum = jnp.zeros((rows, 1), f32)
    target = jnp.zeros((rows, 1), f32)
    for s in range(n):
        got = e_recv[s]
        exp_sum += got[:, 1:2] * jnp.exp(got[:, :1] - top)
        target += got[:, 2:3]
    result = jnp.broadcast_to(target - top - jnp.log(exp_sum), (rows, HEAD_SIZE))
    diagonal = lax.broadcasted_iota(jnp.int32, (rows, HEAD_SIZE), 0) == lane
    log_probs[...] = jnp.sum(jnp.where(diagonal, result, 0.0), axis=0, keepdims=True)[:, :rows]

    @pl.loop(1, n)
    def _(i):
        to = (me + i) % n
        remote(queries.at[step], q_all.at[me], q_ss.at[i], q_rs.at[me], role, to).wait_send()
        remote(b_send.at[to], b_recv.at[me], b_ss.at[i], b_rs.at[me], role, to).wait_send()
        remote(c_send.at[to], c_recv.at[me], c_ss.at[i], c_rs.at[me], role, to).wait_send()
        remote(
            d_send, d_recv.at[own_slot], d_ss.at[i], d_rs.at[own_slot], target_role, to
        ).wait_send()
        remote(e_send, e_recv.at[me], e_ss.at[i], e_rs.at[me], role, to).wait_send()

    @pl.when(target_role != role)
    def _():
        remote(
            d_send, d_recv.at[own_slot], d_ss.at[0], d_rs.at[own_slot], target_role, me
        ).wait_send()

    @pl.loop(0, n)
    def _(i):
        remote(s_send, s_recv.at[me], s_ss.at[i], s_rs.at[me], 1 - role, me).wait_send()

    remote(x_send, x_recv, x_sem.at[0], x_sem.at[1], 1 - role, me).wait_send()
    for j in range(tiles):
        y_copy(j).wait_send()


def fused(
    queries,
    step_token_keys,
    step_token_values,
    stored_key_cache,
    stored_value_cache,
    lengths,
    wo_sides,
    gain_sides,
    head,
    resid,
    actions,
):
    tp = lax.axis_size("tp")
    n = lax.axis_size("grp") * tp
    rows = lengths.shape[0]
    width = resid.shape[2]
    heads = width // HEAD_SIZE
    depth = head.shape[0] // 2
    tiles = -(-head.shape[1] // TILE)
    bf16, f32 = jnp.bfloat16, jnp.float32
    vmem = pl.BlockSpec(memory_space=pltpu.VMEM)
    smem = pl.BlockSpec(memory_space=pltpu.SMEM)
    hbm = pl.BlockSpec(memory_space=pl.ANY)
    message = heads * rows + 2 * rows
    dma = pltpu.SemaphoreType.DMA
    return pl.pallas_call(
        functools.partial(fused_kernel, n, tp),
        out_shape=(
            jax.ShapeDtypeStruct((1, rows), f32),
            jax.ShapeDtypeStruct((1, rows, width), bf16),
        ),
        in_specs=[vmem, vmem, vmem, hbm, hbm, smem, vmem, vmem, smem, hbm, hbm],
        out_specs=(vmem, vmem),
        scratch_shapes=[
            pltpu.VMEM(stored_key_cache.shape, bf16),
            pltpu.VMEM(stored_value_cache.shape, bf16),
            pltpu.VMEM(wo_sides.shape[1:], bf16),
            pltpu.VMEM((head.shape[1], depth), bf16),
            pltpu.VMEM((n, rows, width), bf16),
            pltpu.VMEM((n, message, HEAD_SIZE), bf16),
            pltpu.VMEM((n, message, HEAD_SIZE), bf16),
            pltpu.VMEM((n, rows, width), bf16),
            pltpu.VMEM((n, rows, width), bf16),
            pltpu.VMEM((rows, width), bf16),
            pltpu.VMEM((n, rows, width), bf16),
            pltpu.VMEM((rows, width), f32),
            pltpu.VMEM((rows, width), f32),
            pltpu.VMEM((rows, HEAD_SIZE), f32),
            pltpu.VMEM((n, rows, HEAD_SIZE), f32),
            pltpu.VMEM((2 * rows, depth), bf16),
            pltpu.VMEM((tiles, rows, TILE), f32),
            pltpu.VMEM((tiles, rows, TILE), f32),
            pltpu.VMEM((tiles, rows, TILE), f32),
            pltpu.VMEM((rows, HEAD_SIZE), f32),
            pltpu.VMEM((n, rows, HEAD_SIZE), f32),
            dma((2,)),
            dma,
            dma((tiles,)),
            dma((n,)),
            dma((n,)),
            dma((n,)),
            dma((n,)),
            dma((n,)),
            dma((n,)),
            dma((n,)),
            dma((n,)),
            dma((2,)),
            dma((n,)),
            dma((n,)),
            dma((tiles,)),
            dma((tiles,)),
            dma((n,)),
            dma((n,)),
        ],
        compiler_params=pltpu.CompilerParams(
            collective_id=0, has_side_effects=True, vmem_limit_bytes=60 * 1024 * 1024
        ),
    )(
        queries,
        step_token_keys,
        step_token_values,
        stored_key_cache,
        stored_value_cache,
        lengths,
        gain_sides,
        resid,
        actions,
        wo_sides,
        head.T,
    )


def on_device(*args):
    queries, lengths, head = args[0], args[5], args[8]
    n = lax.axis_size("grp") * lax.axis_size("tp")
    width = queries.shape[2]
    group = QUERY_HEADS // KEY_VALUE_HEADS
    whole_heads = width % HEAD_SIZE == 0 and group % (width // HEAD_SIZE) == 0
    fits = lax.axis_size("role") == 2 and n % 2 == 0 and lengths.shape[0] == 8
    if whole_heads and fits and head.shape[0] == n * width and head.shape[1] > TILE:
        return fused(*args)
    return plain(*args)


def solution(mesh):
    in_specs = (
        P(None, None, ("grp", "tp")),
        P(),
        P(),
        P(None, ("grp", "tp"), None),
        P(None, ("grp", "tp"), None),
        P(),
        P("role", ("grp", "tp"), None),
        P("role", ("grp", "tp")),
        P(None, ("grp", "tp")),
        P(None, None, ("grp", "tp")),
        P(),
    )
    out_specs = (P("role", None), P("role", None, ("grp", "tp")))
    return jax.shard_map(
        on_device, mesh=mesh, in_specs=in_specs, out_specs=out_specs, check_vma=False
    )
```

profile of v0, /device:TPU:0, one launch (start us, length us, event | category | flops | bytes accessed | tf_op | source)
XLA Modules:
  0.0 56.4 jit_solution(12880741012277194088)
XLA Ops:
  0.6 53.3 %shard_map.122 = (f32[1,8]{1,0:T(1,128)}, bf16[1,8,512]{2,1,0:T(8,128)(2,1)}) custom-call(bf16[2,8,512]{2,1,0:T(8,128)(2,1)} %queries.1, bf16[2,8,1024]{2,1,0:T(8,128)(2,1)} %token_keys.1, bf16[2,8,1024]{2,1,0:T(8,128)(2,1)} %token_values.1, bf16[8,32,1024]{2,1,0:T(8,128)(2,1)} %keys_in.1, bf16[8,32,1024]{2,1,0:T(8,128)(2,1)} %values_in.1, s32[8]{0:T(128)} %lengths.1, ...), custom_call_target="tpu_custom_call" | custom-call | tf_op jit(solution)/shard_map/pallas_call | solution.py:576
  54.0 1.1 %copy.15 = f32[1,8]{1,0:T(1,128)} copy(f32[1,8]{1,0:T(1,128)} %get-tuple-element.4) | data formatting | bytes 64
  55.1 1.3 %copy.16 = bf16[1,8,512]{2,1,0:T(8,128)(2,1)} copy(bf16[1,8,512]{2,1,0:T(8,128)(2,1)} %get-tuple-element.5) | data formatting | bytes 16384
where the time goes:
time: 56.6 us; the launch traced here: 56.4 us
  Pallas kernels  53.3 us (94%)
  local copies, waits for them, and re-layouts  2.43 us (4%)
  between operations  0.64 us (1%)
    pallas_call x1, Pallas kernels, fused(): pl.pallas_call(functools.partial(fused_kernel, n, tp), out_shape=(jax.Sha...  53.3 us
    unnamed x2, local copies, waits for them, and re-layouts  2.43 us

commit v1 on v0

v1 whole, which is shorter than its diff:
```python
import functools
import math

import jax
import jax.numpy as jnp
from jax import lax
from jax.experimental import pallas as pl
from jax.experimental.pallas import tpu as pltpu
from jax.sharding import PartitionSpec as P

D = 8192
QUERY_HEADS = 64
KEY_VALUE_HEADS = 8
HEAD_SIZE = 128
DECODE_STEPS = 2


def swap_sides(value):
    return lax.ppermute(value, "role", [(0, 1), (1, 0)])


def plain(
    queries,
    step_token_keys,
    step_token_values,
    stored_key_cache,
    stored_value_cache,
    lengths,
    wo_sides,
    gain_sides,
    head,
    resid,
    actions,
):
    both = ("grp", "tp")
    place = lax.axis_index(both)
    step = 1 - lax.axis_index("role")
    count_of_rows = lengths.shape[0]
    shard_length = stored_key_cache.shape[1]
    query_group_width = QUERY_HEADS // KEY_VALUE_HEADS
    logit_scale = 1.0 / math.sqrt(HEAD_SIZE)
    query_matrix = lax.all_gather(
        lax.dynamic_index_in_dim(queries, step, 0, keepdims=False), both, axis=1, tiled=True
    )
    positions = place * shard_length + jnp.arange(shard_length, dtype=jnp.int32)
    valid = positions[None, :] < lengths[:, None]
    masking = valid[:, None, None, :]
    cache_shape = (count_of_rows, shard_length, KEY_VALUE_HEADS, HEAD_SIZE)
    prior_keys = stored_key_cache.reshape(cache_shape)
    prior_values = stored_value_cache.reshape(cache_shape)
    step_shape = (DECODE_STEPS, count_of_rows, KEY_VALUE_HEADS, HEAD_SIZE)
    incoming_keys = step_token_keys.astype(jnp.float32).reshape(step_shape)
    incoming_values = step_token_values.astype(jnp.float32).reshape(step_shape)
    current_query = query_matrix.reshape(
        count_of_rows, KEY_VALUE_HEADS, query_group_width, HEAD_SIZE
    )
    scores = (
        jnp.einsum("rkgd,rskd->rkgs", current_query, prior_keys, preferred_element_type=jnp.float32)
        * logit_scale
    )
    scores = jnp.where(masking, scores, -1e30)
    fresh_live = jnp.arange(DECODE_STEPS, dtype=jnp.int32) <= step
    fresh_scores = (
        jnp.einsum("rkgd,trkd->rkgt", current_query.astype(jnp.float32), incoming_keys)
        * logit_scale
    )
    fresh_scores = jnp.where(fresh_live, fresh_scores, -1e30)
    fresh_highest = jnp.max(fresh_scores, axis=-1)
    overall = lax.pmax(jnp.maximum(jnp.max(scores, axis=-1), fresh_highest), both)
    cache_probs = jnp.exp(scores - overall[..., None]) * masking
    fresh_probs = jnp.exp(fresh_scores - overall[..., None]) * fresh_live
    fresh_probs = fresh_probs * (place == 0)
    totals = jnp.sum(cache_probs, axis=-1) + jnp.sum(fresh_probs, axis=-1)
    weighted = jnp.einsum(
        "rkgs,rskd->rkgd", cache_probs, prior_values.astype(jnp.float32)
    ) + jnp.einsum("rkgt,trkd->rkgd", fresh_probs, incoming_values)
    features = QUERY_HEADS * HEAD_SIZE
    mixed = lax.psum_scatter(
        weighted.reshape(count_of_rows, features), both, scatter_dimension=1, tiled=True
    )
    totals = lax.psum(totals.reshape(count_of_rows, QUERY_HEADS), both)
    feature_rows = wo_sides.shape[1]
    own_heads = (place * feature_rows + jnp.arange(feature_rows)) // HEAD_SIZE
    own_part = (mixed / jnp.take(totals, own_heads, axis=1)).astype(jnp.bfloat16)
    branch_out = lax.psum_scatter(
        jnp.dot(own_part, wo_sides[0], preferred_element_type=jnp.float32),
        both,
        scatter_dimension=1,
        tiled=True,
    )
    resid_now = lax.dynamic_index_in_dim(resid, step, 0, keepdims=False)
    state = resid_now.astype(jnp.float32) + branch_out
    square_sum = lax.psum(jnp.sum(state * state, axis=-1), both)
    normed_now = (
        state * lax.rsqrt(square_sum[:, None] / D + 1e-05) * gain_sides[0][None, :]
    ).astype(jnp.bfloat16)
    logits = jnp.dot(
        lax.all_gather(normed_now, both, axis=1, tiled=True),
        head,
        preferred_element_type=jnp.float32,
    )
    local_highest = jnp.max(logits, axis=-1)
    action_now = lax.dynamic_index_in_dim(actions, step, 0, keepdims=False)
    head_width = head.shape[1]
    vocab_ids = place * head_width + jnp.arange(head_width, dtype=jnp.int32)
    is_target = vocab_ids[None, :] == action_now[:, None]
    target = jnp.sum(jnp.where(is_target, logits, 0.0), axis=-1)
    exp_sum = jnp.sum(jnp.exp(logits - local_highest[:, None]), axis=-1)
    parts = lax.all_gather(jnp.stack([local_highest, exp_sum, target]), both)
    largest = jnp.max(parts[:, 0], axis=0)
    exp_sum = jnp.sum(parts[:, 1] * jnp.exp(parts[:, 0] - largest[None]), axis=0)
    prob_now = jnp.sum(parts[:, 2], axis=0) - largest - jnp.log(exp_sum)
    return (swap_sides(prob_now)[None], swap_sides(normed_now)[None])


LOW = -1e30
DEAD = -1e29
TILE = 256
MESH = pl.DeviceIdType.MESH


def fused_kernel(
    n,
    tp,
    queries,
    token_keys,
    token_values,
    keys_in,
    values_in,
    lengths_in,
    gain_in,
    resid_in,
    actions_in,
    wo,
    head,
    log_probs,
    normed,
    q_own,
    fresh_keys,
    fresh_values,
    lengths,
    actions,
    gain,
    resid,
    keys,
    values,
    wo_buf,
    head_buf,
    bias,
    q_all,
    b_send,
    b_recv,
    c_send,
    c_recv,
    x_all,
    s_send,
    s_recv,
    acc,
    n_send,
    n_recv,
    e_send,
    e_recv,
    in_sems,
    head_sems,
    q_ss,
    q_rs,
    k_ss,
    k_rs,
    b_ss,
    b_rs,
    c_ss,
    c_rs,
    d_ss,
    f_ss,
    x_rs,
    s_ss,
    s_rs,
    n_sems,
    e_ss,
    e_rs,
):
    role = lax.axis_index("role")
    me = lax.axis_index("grp") * tp + lax.axis_index("tp")
    core = me % 2
    chip = me // 2
    mate = me + 1 - 2 * core
    chips = n // 2
    near = chips // 2
    half = n // 2
    side = chip // near
    step = 1 - role
    rows = resid.shape[0]
    width = resid.shape[1]
    shard = keys.shape[2]
    half_keys = keys.shape[3]
    own_heads = width // HEAD_SIZE
    group = QUERY_HEADS // KEY_VALUE_HEADS
    slots = 2 * rows * shard
    vocab = head.shape[0]
    kept = head_buf.shape[0]
    tiles = acc.shape[0]
    scale = 1.0 / math.sqrt(HEAD_SIZE)
    f32 = jnp.float32
    bf16 = jnp.bfloat16

    def flip(index, by, size):
        out = index
        bit = 1
        while bit < size:
            if isinstance(by, int):
                if by // bit % 2:
                    out = out + bit - 2 * bit * (index // bit % 2)
            else:
                out = out + (by // bit % 2) * (bit - 2 * bit * (index // bit % 2))
            bit *= 2
        return out

    def remote(src, dst, ss, rs, to_role, place):
        return pltpu.make_async_remote_copy(
            src_ref=src,
            dst_ref=dst,
            send_sem=ss,
            recv_sem=rs,
            device_id=(to_role, place // tp, place % tp),
            device_id_type=MESH,
        )

    def landed(ref, sem):
        pltpu.make_async_copy(ref, ref, sem).wait()

    own_keys = pl.ds(pl.multiple_of(core * half_keys, 128), half_keys)
    mate_keys = pl.ds(pl.multiple_of((1 - core) * half_keys, 128), half_keys)
    chip_lanes = pl.ds(pl.multiple_of(chip * HEAD_SIZE, HEAD_SIZE), HEAD_SIZE)
    loads = [
        pltpu.make_async_copy(src, dst, in_sems.at[i])
        for i, (src, dst) in enumerate(
            [
                (queries.at[step], q_own),
                (lengths_in, lengths),
                (keys_in.at[:, :, own_keys], keys.at[core]),
                (values_in.at[:, :, own_keys], values.at[core]),
                (token_keys.at[:, :, chip_lanes], fresh_keys),
                (token_values.at[:, :, chip_lanes], fresh_values),
                (resid_in.at[step], resid),
                (gain_in, gain),
                (actions_in, actions),
                (wo.at[0], wo_buf),
            ]
        )
    ]
    for copy in loads:
        copy.start()
    first_row = pl.multiple_of(role * (vocab - kept), 8)

    def head_copy(p):
        lanes = pl.ds(pl.multiple_of(p * width, 128), width)
        return pltpu.make_async_copy(
            head.at[pl.ds(first_row, kept), lanes], head_buf.at[:, lanes], head_sems.at[p]
        )

    @pl.loop(0, n)
    def _(p):
        head_copy(p).start()

    barrier = pltpu.get_barrier_semaphore()
    for i in range(1, 2 * n):
        other = (role * n + me + i) % (2 * n)
        pl.semaphore_signal(
            barrier,
            inc=1,
            device_id=(other // n, other % n // tp, other % tp),
            device_id_type=MESH,
        )
    loads[0].wait()
    pl.semaphore_wait(barrier, 2 * n - 1)

    own_slot = me % half
    for i in range(chips - 1, 0, -1):
        to = 2 * flip(chip, i, chips) + side
        remote(q_own, q_all.at[own_slot], q_ss.at[i], q_rs.at[own_slot], role, to).start()

    @pl.when(core != side)
    def _():
        remote(q_own, q_all.at[own_slot], q_ss.at[0], q_rs.at[own_slot], role, mate).start()

    @pl.when(core == side)
    def _():
        q_all[own_slot] = q_own[...]

    key_swap = remote(
        keys_in.at[:, :, mate_keys], keys.at[core], k_ss.at[0], k_rs.at[0], role, mate
    )
    value_swap = remote(
        values_in.at[:, :, mate_keys], values.at[core], k_ss.at[1], k_rs.at[1], role, mate
    )
    key_swap.start()
    value_swap.start()

    loads[1].wait()
    row_ids = lax.broadcasted_iota(jnp.int32, (rows, slots), 0)
    col_ids = lax.broadcasted_iota(jnp.int32, (rows, slots), 1)
    limit = jnp.zeros((rows, slots), jnp.int32)
    for b in range(rows):
        limit = jnp.where(row_ids == b, lengths[b], limit)
    origin = col_ids // (rows * shard)
    place_ids = (2 * chip + origin) * shard + col_ids % shard
    live = (col_ids // shard % rows == row_ids) & (place_ids < limit)
    bias[...] = jnp.where(live, 0.0, LOW)

    loads[2].wait()
    loads[3].wait()
    ones = jnp.ones((slots, HEAD_SIZE), bf16)
    lane = lax.broadcasted_iota(jnp.int32, (rows, HEAD_SIZE), 1)

    def wait_query(slot):
        remote(q_own, q_all.at[slot], q_ss.at[0], q_rs.at[slot], role, me).wait_recv()

    for i in range(near):
        local = flip(chip % near, i, near)
        slot = 2 * local
        if i == 0:

            @pl.when(core == side)
            def _():
                wait_query(mate % half)

            @pl.when(core != side)
            def _():
                wait_query(slot)
                wait_query(slot + 1)

            remote(
                keys_in.at[:, :, mate_keys], keys.at[1 - core], k_ss.at[0], k_rs.at[0], role, me
            ).wait_recv()
            remote(
                values_in.at[:, :, mate_keys], values.at[1 - core], k_ss.at[1], k_rs.at[1], role, me
            ).wait_recv()
        else:
            wait_query(slot)
            wait_query(slot + 1)
        lanes = pl.ds(pl.multiple_of(local * HEAD_SIZE, HEAD_SIZE), HEAD_SIZE)
        query = jnp.concatenate(
            [
                q_all[slot + part, :, j * HEAD_SIZE : (j + 1) * HEAD_SIZE].astype(f32)
                for part in range(2)
                for j in range(own_heads)
            ],
            axis=0,
        ).astype(bf16)
        key = keys[:, :, :, lanes].reshape(slots, HEAD_SIZE)
        value = values[:, :, :, lanes].reshape(slots, HEAD_SIZE)
        scores = lax.dot_general(query, key, (((1,), (1,)), ((), ())), preferred_element_type=f32)
        scores = (scores * scale).reshape(group, rows, slots) + bias[...][None]
        scores = scores.reshape(group * rows, slots)
        top = jnp.max(scores, axis=1, keepdims=True)
        top = jnp.maximum(top, DEAD).astype(bf16).astype(f32)
        probs = jnp.exp(scores - top).astype(bf16)
        both = jnp.dot(
            probs, jnp.concatenate([value, ones], axis=1), preferred_element_type=f32
        )
        weighted = both[:, :HEAD_SIZE]
        total = both[:, HEAD_SIZE:]
        total_high = total.astype(bf16).astype(f32)
        total_low = total - total_high
        for part in range(2):
            stats = jnp.zeros((rows, HEAD_SIZE), f32)
            for j in range(own_heads):
                at = (part * own_heads + j) * rows
                stats = jnp.where(lane == j, top[at : at + rows], stats)
                stats = jnp.where(lane == own_heads + j, total_high[at : at + rows], stats)
                stats = jnp.where(lane == 2 * own_heads + j, total_low[at : at + rows], stats)
            first = part * own_heads * rows
            b_send[slot + part] = jnp.concatenate(
                [weighted[first : first + own_heads * rows], stats], axis=0
            ).astype(bf16)
        for part in range(2):
            to = core * half + slot + part
            copy = remote(
                b_send.at[slot + part], b_recv.at[chip], b_ss.at[2 * i + part], b_rs, role, to
            )
            if i == 0:

                @pl.when(to != me)
                def _(copy=copy):
                    copy.start()

                @pl.when(to == me)
                def _(part=part):
                    b_recv[chip] = b_send[slot + part]

            else:
                copy.start()

    for copy in loads[4:9]:
        copy.wait()
    own_query = q_own[...].astype(f32)
    fresh = []
    for u in range(DECODE_STEPS):
        fresh_key = fresh_keys[u].astype(f32)
        fresh.append(
            [
                jnp.where(
                    u <= step,
                    jnp.sum(
                        own_query[:, j * HEAD_SIZE : (j + 1) * HEAD_SIZE] * fresh_key,
                        axis=1,
                        keepdims=True,
                    )
                    * scale,
                    LOW,
                )
                for j in range(own_heads)
            ]
        )

    @pl.when(core == side)
    def _():
        landed(b_recv.at[pl.ds(0, chips - 1)], b_rs)

    @pl.when(core != side)
    def _():
        landed(b_recv, b_rs)

    stats = [b_recv[s, own_heads * rows :, :].astype(f32) for s in range(chips)]
    top = functools.reduce(jnp.maximum, stats)
    tops = [
        functools.reduce(
            jnp.maximum, [fresh[u][j] for u in range(DECODE_STEPS)], top[:, j : j + 1]
        )
        for j in range(own_heads)
    ]
    numerator = [jnp.zeros((rows, HEAD_SIZE), f32) for _ in range(own_heads)]
    denominator = [jnp.zeros((rows, 1), f32) for _ in range(own_heads)]
    for j in range(own_heads):
        for u in range(DECODE_STEPS):
            weight = jnp.where(u <= step, jnp.exp(fresh[u][j] - tops[j]), 0.0)
            numerator[j] += weight * fresh_values[u].astype(f32)
            denominator[j] += weight
    for s in range(chips):
        part = b_recv[s, : own_heads * rows, :].astype(f32)
        for j in range(own_heads):
            factor = jnp.exp(stats[s][:, j : j + 1] - tops[j])
            numerator[j] += factor * part[j * rows : (j + 1) * rows]
            at = own_heads + j
            denominator[j] += factor * (
                stats[s][:, at : at + 1] + stats[s][:, at + own_heads : at + own_heads + 1]
            )
    attended = jnp.concatenate(
        [numerator[j] / denominator[j] for j in range(own_heads)], axis=1
    ).astype(bf16)

    loads[9].wait()
    block = 4
    for i in range(n // block - 1, -1, -1):
        base = flip(me // block, i, n // block) * block
        out = jnp.dot(
            attended,
            wo_buf[:, pl.ds(pl.multiple_of(base * width, 128), block * width)],
            preferred_element_type=f32,
        )
        for j in range(block):
            c_send[base + j] = out[:, j * width : (j + 1) * width].astype(bf16)
        for j in range(block):
            to = base + j
            copy = remote(c_send.at[to], c_recv.at[me], c_ss, c_rs, role, to)
            if i == 0:

                @pl.when(to != me)
                def _(copy=copy):
                    copy.start()

            else:
                copy.start()
    state = resid[...].astype(f32)
    c_recv[me] = c_send[me]

    landed(c_recv.at[pl.ds(0, n - 1)], c_rs)
    for s in range(n):
        state += c_recv[s].astype(f32)

    def slot_of(from_role, place):
        return 2 * place + 1 - from_role

    mine = slot_of(role, me)
    x_all[mine] = (state * gain[...]).astype(bf16)

    def x_copy(slot, rs, ss, to_role, to):
        return remote(x_all.at[slot], x_all.at[slot], ss, rs, to_role, to)

    for i in range(chips - 1, -1, -1):
        to = 2 * flip(chip, i, chips) + core
        x_copy(mine, x_rs.at[mine], d_ss, 1 - role, to).start()
        if i:
            x_copy(mine, x_rs.at[mine], d_ss, role, to).start()
    x_copy(mine, x_rs.at[mine], d_ss, role, mate).start()

    diagonal = lax.broadcasted_iota(jnp.int32, (rows, HEAD_SIZE), 0)
    square = jnp.sum(state * state, axis=1, keepdims=True)
    s_send[...] = jnp.sum(jnp.where(diagonal == lane, square, 0.0), axis=0, keepdims=True)
    own_stat = role * n + me
    for i in range(n - 1, -1, -1):
        to = flip(me, i, n)
        remote(s_send, s_recv.at[own_stat], s_ss, s_rs, 1 - role, to).start()
        if i:
            remote(s_send, s_recv.at[own_stat], s_ss, s_rs, role, to).start()
    s_recv[own_stat] = s_send[...]

    @pl.loop(0, n)
    def _(p):
        head_copy(p).wait()

    def wait_x(slot):
        x_copy(slot, x_rs.at[slot], d_ss, role, me).wait_recv()

    def chunk(place, start):
        x = jnp.concatenate(
            [x_all[2 * place].astype(f32), x_all[2 * place + 1].astype(f32)], axis=0
        ).astype(bf16)
        lanes = pl.ds(pl.multiple_of(place * width, 128), width)
        for t in range(tiles):
            size = min(TILE, kept - t * TILE)
            y = lax.dot_general(
                x,
                head_buf[t * TILE : t * TILE + size, lanes],
                (((1,), (1,)), ((), ())),
                preferred_element_type=f32,
            )
            if start:
                acc[t, :, :size] = y
            else:
                acc[t, :, :size] += y

    def take(slot):
        wait_x(slot)
        x_copy(slot, x_rs.at[slot], f_ss, role, mate).start()

    take(slot_of(1 - role, me))
    chunk(me, True)

    @pl.loop(1, chips)
    def _(i):
        place = 2 * flip(chip, i, chips) + core
        take(2 * place)
        take(2 * place + 1)
        chunk(place, False)
        place = 2 * flip(chip, i - 1, chips) + 1 - core
        wait_x(2 * place)
        wait_x(2 * place + 1)
        chunk(place, False)

    last = 2 * flip(chip, chips - 1, chips) + 1 - core
    wait_x(2 * last)
    wait_x(2 * last + 1)
    chunk(last, False)

    landed(s_recv.at[pl.ds(0, 2 * n - 1)], s_rs)
    inverse = []
    for t in range(DECODE_STEPS):
        square = functools.reduce(jnp.add, [s_recv[(1 - t) * n + s] for s in range(n)])
        factor = lax.rsqrt(square / (n * width) + 1e-05)
        inverse.append(
            jnp.sum(jnp.where(diagonal == lane, factor, 0.0), axis=1, keepdims=True)
        )
    own_inverse = jnp.where(role == 0, inverse[1], inverse[0])
    inverse = jnp.concatenate(inverse, axis=0)
    n_send[...] = (state * own_inverse * gain[...]).astype(bf16)
    n_copy = remote(n_send, n_recv, n_sems.at[0], n_sems.at[1], 1 - role, me)
    n_copy.start()

    action_rows = lax.broadcasted_iota(jnp.int32, (2 * rows, 1), 0)
    action = jnp.zeros((2 * rows, 1), jnp.int32)
    for t in range(DECODE_STEPS):
        for b in range(rows):
            action = jnp.where(action_rows == t * rows + b, actions[t, b], action)
    wanted = action - (me * vocab + first_row)
    twice = role * (2 * kept - vocab)
    tile_ids = lax.broadcasted_iota(jnp.int32, (2 * rows, TILE), 1)
    largest = jnp.full((2 * rows, 1), LOW, f32)
    logits = []
    for t in range(tiles):
        size = min(TILE, kept - t * TILE)
        tile = acc[t, :, :size] * inverse
        if t == 0:
            tile = jnp.where(tile_ids[:, :size] < twice, LOW, tile)
        logits.append(tile)
    whole = [tile for tile in logits if tile.shape[1] == TILE]
    largest = jnp.max(functools.reduce(jnp.maximum, whole), axis=1, keepdims=True)
    for tile in logits:
        if tile.shape[1] != TILE:
            largest = jnp.maximum(largest, jnp.max(tile, axis=1, keepdims=True))
    exp_sum = jnp.zeros((2 * rows, 1), f32)
    target = jnp.zeros((2 * rows, 1), f32)
    whole_sum = jnp.zeros((2 * rows, TILE), f32)
    whole_target = jnp.zeros((2 * rows, TILE), f32)
    for t, tile in enumerate(logits):
        size = tile.shape[1]
        here = tile_ids[:, :size] + t * TILE == wanted
        if t == 0:
            here = here & (tile_ids[:, :size] >= twice)
        power = jnp.exp(tile - largest)
        hit = jnp.where(here, tile, 0.0)
        if size == TILE:
            whole_sum += power
            whole_target += hit
        else:
            exp_sum += jnp.sum(power, axis=1, keepdims=True)
            target += jnp.sum(hit, axis=1, keepdims=True)
    exp_sum += jnp.sum(whole_sum, axis=1, keepdims=True)
    target += jnp.sum(whole_target, axis=1, keepdims=True)
    for t in range(DECODE_STEPS):
        part = slice(t * rows, (t + 1) * rows)
        packed = jnp.where(lane == diagonal, largest[part], 0.0)
        packed = jnp.where(lane == diagonal + rows, exp_sum[part], packed)
        packed = jnp.where(lane == diagonal + 2 * rows, target[part], packed)
        e_send[t] = jnp.sum(packed, axis=0, keepdims=True)
    for i in range(n - 1, -1, -1):
        to = flip(me, i, n)
        remote(e_send.at[1 - role], e_recv.at[own_stat], e_ss, e_rs, 1 - role, to).start()
        if i:
            remote(e_send.at[role], e_recv.at[own_stat], e_ss, e_rs, role, to).start()
    e_recv[own_stat] = e_send[role]

    n_copy.wait_recv()
    out_copy = pltpu.make_async_copy(n_recv, normed.at[0], n_sems.at[2])
    out_copy.start()
    n_copy.wait_send()
    for i in range(1, chips):
        remote(q_own, q_all.at[own_slot], q_ss.at[i], q_rs.at[own_slot], role, me).wait_send()

    @pl.when(core != side)
    def _():
        remote(q_own, q_all.at[own_slot], q_ss.at[0], q_rs.at[own_slot], role, mate).wait_send()

    key_swap.wait_send()
    value_swap.wait_send()
    for i in range(near):
        for part in range(2):
            copy = remote(
                b_send.at[0], b_recv.at[chip], b_ss.at[2 * i + part], b_rs, role, me
            )
            if i == 0:

                @pl.when(core * half + 2 * (chip % near) + part != me)
                def _(copy=copy):
                    copy.wait_send()

            else:
                copy.wait_send()
    landed(c_send.at[pl.ds(0, n - 1)], c_ss)
    landed(x_all.at[pl.ds(0, n)], d_ss)
    landed(x_all.at[pl.ds(0, n - 1)], f_ss)
    landed(s_recv.at[pl.ds(0, 2 * n - 1)], s_ss)

    landed(e_recv.at[pl.ds(0, 2 * n - 1)], e_rs)
    got = [e_recv[s] for s in range(2 * n)]
    top = functools.reduce(jnp.maximum, got)
    exp_sum = jnp.zeros((1, HEAD_SIZE), f32)
    target = jnp.zeros((1, HEAD_SIZE), f32)
    stack = jnp.concatenate(got, axis=0)
    factor = pltpu.roll(jnp.exp(stack - top), rows, 1)
    exp_sum = jnp.sum(stack * factor, axis=0, keepdims=True)
    target = jnp.sum(stack, axis=0, keepdims=True)
    exp_sum = pltpu.roll(exp_sum, HEAD_SIZE - rows, 1)
    target = pltpu.roll(target, HEAD_SIZE - 2 * rows, 1)
    log_probs[...] = (target - top - jnp.log(exp_sum))[:, :rows]
    landed(e_recv.at[pl.ds(0, 2 * n - 1)], e_ss)
    out_copy.wait()


def fused(
    queries,
    step_token_keys,
    step_token_values,
    stored_key_cache,
    stored_value_cache,
    lengths,
    wo_sides,
    gain_sides,
    head,
    resid,
    actions,
):
    tp = lax.axis_size("tp")
    n = lax.axis_size("grp") * tp
    rows = lengths.shape[0]
    width = resid.shape[2]
    heads = width // HEAD_SIZE
    kept = -(-head.shape[1] // 16) * 8
    tiles = -(-kept // TILE)
    shard = stored_key_cache.shape[1]
    slots = 2 * rows * shard
    half_keys = stored_key_cache.shape[2] // 2
    bf16, f32 = jnp.bfloat16, jnp.float32
    vmem = pl.BlockSpec(memory_space=pltpu.VMEM)
    hbm = pl.BlockSpec(memory_space=pl.ANY)
    message = heads * rows + rows
    dma = pltpu.SemaphoreType.DMA
    return pl.pallas_call(
        functools.partial(fused_kernel, n, tp),
        out_shape=(
            jax.ShapeDtypeStruct((1, rows), f32),
            jax.ShapeDtypeStruct((1, rows, width), bf16),
        ),
        in_specs=[hbm] * 11,
        out_specs=(vmem, hbm),
        scratch_shapes=[
            pltpu.VMEM((rows, width), bf16),
            pltpu.VMEM((DECODE_STEPS, rows, HEAD_SIZE), bf16),
            pltpu.VMEM((DECODE_STEPS, rows, HEAD_SIZE), bf16),
            pltpu.SMEM((rows,), jnp.int32),
            pltpu.SMEM((DECODE_STEPS, rows), jnp.int32),
            pltpu.VMEM((1, width), f32),
            pltpu.VMEM((rows, width), bf16),
            pltpu.VMEM((2, rows, shard, half_keys), bf16),
            pltpu.VMEM((2, rows, shard, half_keys), bf16),
            pltpu.VMEM(wo_sides.shape[1:], bf16),
            pltpu.VMEM((kept, head.shape[0]), bf16),
            pltpu.VMEM((rows, slots), f32),
            pltpu.VMEM((n // 2, rows, width), bf16),
            pltpu.VMEM((n // 2, message, HEAD_SIZE), bf16),
            pltpu.VMEM((n // 2, message, HEAD_SIZE), bf16),
            pltpu.VMEM((n, rows, width), bf16),
            pltpu.VMEM((n, rows, width), bf16),
            pltpu.VMEM((2 * n, rows, width), bf16),
            pltpu.VMEM((1, HEAD_SIZE), f32),
            pltpu.VMEM((2 * n, 1, HEAD_SIZE), f32),
            pltpu.VMEM((tiles, 2 * rows, TILE), f32),
            pltpu.VMEM((rows, width), bf16),
            pltpu.VMEM((rows, width), bf16),
            pltpu.VMEM((2, 1, HEAD_SIZE), f32),
            pltpu.VMEM((2 * n, 1, HEAD_SIZE), f32),
            dma((10,)),
            dma((n,)),
            dma((n // 2,)),
            dma((n // 2,)),
            dma((2,)),
            dma((2,)),
            dma((n // 2,)),
            dma,
            dma,
            dma,
            dma,
            dma,
            dma((2 * n,)),
            dma,
            dma,
            dma((3,)),
            dma,
            dma,
        ],
        compiler_params=pltpu.CompilerParams(
            collective_id=0, has_side_effects=True, vmem_limit_bytes=60 * 1024 * 1024
        ),
    )(
        queries,
        step_token_keys,
        step_token_values,
        stored_key_cache,
        stored_value_cache,
        lengths,
        gain_sides,
        resid,
        actions,
        wo_sides,
        head.T,
    )


def on_device(*args):
    queries, lengths, head = args[0], args[5], args[8]
    tp = lax.axis_size("tp")
    n = lax.axis_size("grp") * tp
    width = queries.shape[2]
    group = QUERY_HEADS // KEY_VALUE_HEADS
    whole_heads = width % HEAD_SIZE == 0 and 2 * (width // HEAD_SIZE) == group
    powers = n & (n - 1) == 0 and n >= 8 and tp % 2 == 0 and n // 2 == KEY_VALUE_HEADS
    fits = lax.axis_size("role") == 2 and powers and lengths.shape[0] == 8
    if whole_heads and fits and head.shape[0] == n * width and head.shape[1] % 8 == 0:
        return fused(*args)
    return plain(*args)


def solution(mesh):
    in_specs = (
        P(None, None, ("grp", "tp")),
        P(),
        P(),
        P(None, ("grp", "tp"), None),
        P(None, ("grp", "tp"), None),
        P(),
        P("role", ("grp", "tp"), None),
        P("role", ("grp", "tp")),
        P(None, ("grp", "tp")),
        P(None, None, ("grp", "tp")),
        P(),
    )
    out_specs = (P("role", None), P("role", None, ("grp", "tp")))
    return jax.shard_map(
        on_device, mesh=mesh, in_specs=in_specs, out_specs=out_specs, check_vma=False
    )
```

time: 56.6 us -> 44.7 us (0.79)
  Pallas kernels: 53.3 us -> 41.4 us
    pallas_call x1, Pallas kernels: 53.3 us -> 41.4 us  [fused(): pl.pallas_call(functools.partial(fused_kernel, n, tp), out_shape=(jax.Sha...]
where the time goes in v1:
time: 44.7 us; the launch traced here: 44.5 us
  Pallas kernels  41.4 us (93%)
  local copies, waits for them, and re-layouts  2.43 us (5%)
  between operations  0.64 us (1%)
    pallas_call x1, Pallas kernels, fused(): pl.pallas_call(functools.partial(fused_kernel, n, tp), out_shape=(jax.Sha...  41.4 us
    unnamed x2, local copies, waits for them, and re-layouts  2.43 us

profile of v1, /device:TPU:0, one launch (start us, length us, event | category | flops | bytes accessed | tf_op | source)
XLA Modules:
  0.0 44.5 jit_solution(17622375692783286089)
XLA Ops:
  0.6 41.4 %shard_map.122 = (f32[1,8]{1,0:T(1,128)}, bf16[1,8,512]{2,1,0:T(8,128)(2,1)}) custom-call(bf16[2,8,512]{2,1,0:T(8,128)(2,1)} %queries.1, bf16[2,8,1024]{2,1,0:T(8,128)(2,1)} %token_keys.1, bf16[2,8,1024]{2,1,0:T(8,128)(2,1)} %token_values.1, bf16[8,32,1024]{2,1,0:T(8,128)(2,1)} %keys_in.1, bf16[8,32,1024]{2,1,0:T(8,128)(2,1)} %values_in.1, s32[8]{0:T(128)} %lengths_in.1, ...), custom_call_target="tpu_custom_call" | custom-call | tf_op jit(solution)/shard_map/pallas_call | solution.py:698
  42.0 1.1 %copy.15 = f32[1,8]{1,0:T(1,128)} copy(f32[1,8]{1,0:T(1,128)} %get-tuple-element.4) | data formatting | bytes 64
  43.2 1.3 %copy.16 = bf16[1,8,512]{2,1,0:T(8,128)(2,1)} copy(bf16[1,8,512]{2,1,0:T(8,128)(2,1)} %get-tuple-element.5) | data formatting | bytes 16384

commit v2 on v1

--- a/solution.py
+++ b/solution.py
@@ -116,6 +116,8 @@
 LOW = -1e30
 DEAD = -1e29
 TILE = 256
+SINGLE = 3
+TURNS = (3, 3, 5, 3, 2)
 MESH = pl.DeviceIdType.MESH
 
 
@@ -145,7 +147,9 @@
     keys,
     values,
     wo_buf,
-    head_buf,
+    near_head,
+    far_head,
+    turned,
     bias,
     q_all,
     b_send,
@@ -197,7 +201,7 @@
     group = QUERY_HEADS // KEY_VALUE_HEADS
     slots = 2 * rows * shard
     vocab = head.shape[0]
-    kept = head_buf.shape[0]
+    kept = -(-vocab // 16) * 8
     tiles = acc.shape[0]
     scale = 1.0 / math.sqrt(HEAD_SIZE)
     f32 = jnp.float32
@@ -248,20 +252,7 @@
             ]
         )
     ]
-    for copy in loads:
-        copy.start()
-    first_row = pl.multiple_of(role * (vocab - kept), 8)
-
-    def head_copy(p):
-        lanes = pl.ds(pl.multiple_of(p * width, 128), width)
-        return pltpu.make_async_copy(
-            head.at[pl.ds(first_row, kept), lanes], head_buf.at[:, lanes], head_sems.at[p]
-        )
-
-    @pl.loop(0, n)
-    def _(p):
-        head_copy(p).start()
-
+    loads[0].start()
     barrier = pltpu.get_barrier_semaphore()
     for i in range(1, 2 * n):
         other = (role * n + me + i) % (2 * n)
@@ -271,8 +262,44 @@
             device_id=(other // n, other % n // tp, other % tp),
             device_id_type=MESH,
         )
+    for copy in loads[1:-1]:
+        copy.start()
+    first_row = pl.multiple_of(role * (vocab - kept), 8)
+
+    def direct(i):
+        return 2 * flip(chip, i, chips) + core
+
+    def relayed(i):
+        return 2 * flip(chip, i, chips) + 1 - core
+
+    def head_copy(place, buf, i, sem):
+        lanes = pl.ds(pl.multiple_of(place * width, 128), width)
+        return pltpu.make_async_copy(
+            head.at[pl.ds(first_row, kept), lanes], buf.at[i, pl.ds(0, kept), :], head_sems.at[sem]
+        )
+
+    def near_copy(i):
+        return head_copy(direct(i), near_head, i, i)
+
+    def far_copy(i):
+        return head_copy(relayed(i), far_head, i, chips + i)
+
+    @pl.loop(0, TURNS[0])
+    def _(i):
+        near_copy(i).start()
+
+    loads[-1].start()
+
+    @pl.loop(TURNS[0], chips)
+    def _(i):
+        near_copy(i).start()
+
+    @pl.loop(0, chips)
+    def _(i):
+        far_copy(i).start()
+
+    pl.semaphore_wait(barrier, 2 * n - 1)
     loads[0].wait()
-    pl.semaphore_wait(barrier, 2 * n - 1)
 
     own_slot = me % half
     for i in range(chips - 1, 0, -1):
@@ -307,6 +334,29 @@
     live = (col_ids // shard % rows == row_ids) & (place_ids < limit)
     bias[...] = jnp.where(live, 0.0, LOW)
 
+    def turn_one(copy, source, target, i, j):
+        copy(i).wait()
+        for t in range(tiles):
+            size = min(TILE, kept - t * TILE)
+            tile = source[i, t * TILE : t * TILE + size, :].T
+            for k in range(width // TILE):
+                target[j, t * TILE : (t + 1) * TILE, k * TILE : k * TILE + size] = tile[
+                    k * TILE : (k + 1) * TILE
+                ]
+
+    def turn(window):
+        first = sum(TURNS[:window])
+        last = first + TURNS[window]
+
+        @pl.loop(min(first, chips), min(last, chips))
+        def _(i):
+            turn_one(near_copy, near_head, turned, i, i)
+
+        @pl.loop(max(first - chips, 0), max(last - chips, 0))
+        def _(i):
+            turn_one(far_copy, far_head, near_head, i, i)
+
+    turn(0)
     loads[2].wait()
     loads[3].wait()
     ones = jnp.ones((slots, HEAD_SIZE), bf16)
@@ -413,6 +463,8 @@
             ]
         )
 
+    turn(1)
+
     @pl.when(core == side)
     def _():
         landed(b_recv.at[pl.ds(0, chips - 1)], b_rs)
@@ -474,6 +526,7 @@
     state = resid[...].astype(f32)
     c_recv[me] = c_send[me]
 
+    turn(2)
     landed(c_recv.at[pl.ds(0, n - 1)], c_rs)
     for s in range(n):
         state += c_recv[s].astype(f32)
@@ -487,12 +540,12 @@
     def x_copy(slot, rs, ss, to_role, to):
         return remote(x_all.at[slot], x_all.at[slot], ss, rs, to_role, to)
 
-    for i in range(chips - 1, -1, -1):
+    for i in range(chips):
         to = 2 * flip(chip, i, chips) + core
         x_copy(mine, x_rs.at[mine], d_ss, 1 - role, to).start()
-        if i:
-            x_copy(mine, x_rs.at[mine], d_ss, role, to).start()
-    x_copy(mine, x_rs.at[mine], d_ss, role, mate).start()
+        if i == 0:
+            to = mate
+        x_copy(mine, x_rs.at[mine], d_ss, role, to).start()
 
     diagonal = lax.broadcasted_iota(jnp.int32, (rows, HEAD_SIZE), 0)
     square = jnp.sum(state * state, axis=1, keepdims=True)
@@ -505,25 +558,35 @@
             remote(s_send, s_recv.at[own_stat], s_ss, s_rs, role, to).start()
     s_recv[own_stat] = s_send[...]
 
-    @pl.loop(0, n)
-    def _(p):
-        head_copy(p).wait()
+    turn(3)
 
     def wait_x(slot):
         x_copy(slot, x_rs.at[slot], d_ss, role, me).wait_recv()
 
-    def chunk(place, start):
-        x = jnp.concatenate(
+    def features(place):
+        return jnp.concatenate(
             [x_all[2 * place].astype(f32), x_all[2 * place + 1].astype(f32)], axis=0
         ).astype(bf16)
-        lanes = pl.ds(pl.multiple_of(place * width, 128), width)
+
+    def turned_dot(x, ref, i, t, size):
+        return functools.reduce(
+            jnp.add,
+            [
+                jnp.dot(
+                    x[:, k * TILE : (k + 1) * TILE],
+                    ref[i, t * TILE : (t + 1) * TILE, k * TILE : k * TILE + size],
+                    preferred_element_type=f32,
+                )
+                for k in range(width // TILE)
+            ],
+        )
+
+    def add(parts, start=False):
+        terms = [(features(place), ref, i) for place, ref, i in parts]
         for t in range(tiles):
             size = min(TILE, kept - t * TILE)
-            y = lax.dot_general(
-                x,
-                head_buf[t * TILE : t * TILE + size, lanes],
-                (((1,), (1,)), ((), ())),
-                preferred_element_type=f32,
+            y = functools.reduce(
+                jnp.add, [turned_dot(x, ref, i, t, size) for x, ref, i in terms]
             )
             if start:
                 acc[t, :, :size] = y
@@ -534,24 +597,44 @@
         wait_x(slot)
         x_copy(slot, x_rs.at[slot], f_ss, role, mate).start()
 
-    take(slot_of(1 - role, me))
-    chunk(me, True)
-
-    @pl.loop(1, chips)
-    def _(i):
-        place = 2 * flip(chip, i, chips) + core
+    def wait_far(i):
+        place = relayed(i)
+        wait_x(2 * place)
+        wait_x(2 * place + 1)
+
+    def take_direct(i):
+        place = direct(i)
         take(2 * place)
         take(2 * place + 1)
-        chunk(place, False)
-        place = 2 * flip(chip, i - 1, chips) + 1 - core
-        wait_x(2 * place)
-        wait_x(2 * place + 1)
-        chunk(place, False)
-
-    last = 2 * flip(chip, chips - 1, chips) + 1 - core
-    wait_x(2 * last)
-    wait_x(2 * last + 1)
-    chunk(last, False)
+
+    def near_term(i):
+        return direct(i), turned, i
+
+    def far_term(i):
+        return relayed(i), near_head, i
+
+    take(slot_of(1 - role, me))
+    add([near_term(0)], True)
+    turn(4)
+    for i in range(1, SINGLE):
+        take_direct(i)
+        wait_far(i - 1)
+        add([near_term(i), far_term(i - 1)])
+
+    @pl.loop(SINGLE, chips)
+    def _(i):
+        take_direct(i)
+
+    for i in range(SINGLE, chips, 2):
+        for j in range(i, min(i + 2, chips)):
+            wait_far(j - 1)
+        parts = []
+        for j in range(i, min(i + 2, chips)):
+            parts += [near_term(j), far_term(j - 1)]
+        if i + 2 >= chips:
+            wait_far(chips - 1)
+            parts.append(far_term(chips - 1))
+        add(parts)
 
     landed(s_recv.at[pl.ds(0, 2 * n - 1)], s_rs)
     inverse = []
@@ -563,10 +646,6 @@
         )
     own_inverse = jnp.where(role == 0, inverse[1], inverse[0])
     inverse = jnp.concatenate(inverse, axis=0)
-    n_send[...] = (state * own_inverse * gain[...]).astype(bf16)
-    n_copy = remote(n_send, n_recv, n_sems.at[0], n_sems.at[1], 1 - role, me)
-    n_copy.start()
-
     action_rows = lax.broadcasted_iota(jnp.int32, (2 * rows, 1), 0)
     action = jnp.zeros((2 * rows, 1), jnp.int32)
     for t in range(DECODE_STEPS):
@@ -620,9 +699,12 @@
             remote(e_send.at[role], e_recv.at[own_stat], e_ss, e_rs, role, to).start()
     e_recv[own_stat] = e_send[role]
 
+    n_send[...] = (state * own_inverse * gain[...]).astype(bf16)
+    n_copy = remote(n_send, n_recv, n_sems.at[0], n_sems.at[1], 1 - role, me)
+    n_copy.start()
+
     n_copy.wait_recv()
-    out_copy = pltpu.make_async_copy(n_recv, normed.at[0], n_sems.at[2])
-    out_copy.start()
+    normed[0] = n_recv[...]
     n_copy.wait_send()
     for i in range(1, chips):
         remote(q_own, q_all.at[own_slot], q_ss.at[i], q_rs.at[own_slot], role, me).wait_send()
@@ -664,7 +746,17 @@
     target = pltpu.roll(target, HEAD_SIZE - 2 * rows, 1)
     log_probs[...] = (target - top - jnp.log(exp_sum))[:, :rows]
     landed(e_recv.at[pl.ds(0, 2 * n - 1)], e_ss)
-    out_copy.wait()
+
+
+def hand_over(log_probs, normed, log_probs_out, normed_out, sems):
+    copies = [
+        pltpu.make_async_copy(log_probs, log_probs_out, sems.at[0]),
+        pltpu.make_async_copy(normed, normed_out, sems.at[1]),
+    ]
+    for copy in copies:
+        copy.start()
+    for copy in copies:
+        copy.wait()
 
 
 def fused(
@@ -695,14 +787,11 @@
     hbm = pl.BlockSpec(memory_space=pl.ANY)
     message = heads * rows + rows
     dma = pltpu.SemaphoreType.DMA
-    return pl.pallas_call(
+    parts = pl.pallas_call(
         functools.partial(fused_kernel, n, tp),
-        out_shape=(
-            jax.ShapeDtypeStruct((1, rows), f32),
-            jax.ShapeDtypeStruct((1, rows, width), bf16),
-        ),
+        out_shape=(pltpu.VMEM((1, rows), f32), pltpu.VMEM((1, rows, width), bf16)),
         in_specs=[hbm] * 11,
-        out_specs=(vmem, hbm),
+        out_specs=(vmem, vmem),
         scratch_shapes=[
             pltpu.VMEM((rows, width), bf16),
             pltpu.VMEM((DECODE_STEPS, rows, HEAD_SIZE), bf16),
@@ -714,7 +803,9 @@
             pltpu.VMEM((2, rows, shard, half_keys), bf16),
             pltpu.VMEM((2, rows, shard, half_keys), bf16),
             pltpu.VMEM(wo_sides.shape[1:], bf16),
-            pltpu.VMEM((kept, head.shape[0]), bf16),
+            pltpu.VMEM((n // 2, tiles * TILE, width), bf16),
+            pltpu.VMEM((n // 2, tiles * TILE, width), bf16),
+            pltpu.VMEM((n // 2, tiles * TILE, width), bf16),
             pltpu.VMEM((rows, slots), f32),
             pltpu.VMEM((n // 2, rows, width), bf16),
             pltpu.VMEM((n // 2, message, HEAD_SIZE), bf16),
@@ -744,7 +835,7 @@
             dma((2 * n,)),
             dma,
             dma,
-            dma((3,)),
+            dma((2,)),
             dma,
             dma,
         ],
@@ -764,6 +855,13 @@
         wo_sides,
         head.T,
     )
+    return pl.pallas_call(
+        hand_over,
+        out_shape=tuple(jax.ShapeDtypeStruct(part.shape, part.dtype) for part in parts),
+        in_specs=[vmem, vmem],
+        out_specs=(hbm, hbm),
+        scratch_shapes=[dma((2,))],
+    )(*[pltpu.with_memory_space_constraint(part, pltpu.VMEM) for part in parts])
 
 
 def on_device(*args):

time: 44.7 us -> 38 us (0.85)
  Pallas kernels: 41.4 us -> 37.2 us
  local copies, waits for them, and re-layouts: 2.43 us -> 0 us
    pallas_call x1 -> x2, Pallas kernels: 41.4 us -> 37.2 us  [the longest x1 36.6 us: fused(): pl.pallas_call(functools.partial(fused_kernel, n, tp), out_shape=(pltpu.V...]
    unnamed x2 -> x0, local copies, waits for them, and re-layouts: 2.43 us -> none
where the time goes in v2:
time: 38 us; the launch traced here: 37.8 us
  Pallas kernels  37.2 us (98%)
  between operations  0.64 us (2%)
    pallas_call x1, Pallas kernels, fused(): pl.pallas_call(functools.partial(fused_kernel, n, tp), out_shape=(pltpu.V...  36.6 us

profile of v2, /device:TPU:0, one launch (start us, length us, event | category | flops | bytes accessed | tf_op | source)
XLA Modules:
  0.0 37.8 jit_solution(4699289785007648667)
XLA Ops:
  0.6 36.6 %shard_map.122 = (f32[1,8]{1,0:T(1,128)S(1)}, bf16[1,8,512]{2,1,0:T(8,128)(2,1)S(1)}) custom-call(bf16[2,8,512]{2,1,0:T(8,128)(2,1)} %queries.1, bf16[2,8,1024]{2,1,0:T(8,128)(2,1)} %token_keys.1, bf16[2,8,1024]{2,1,0:T(8,128)(2,1)} %token_values.1, bf16[8,32,1024]{2,1,0:T(8,128)(2,1)} %keys_in.1, bf16[8,32,1024]{2,1,0:T(8,128)(2,1)} %values_in.1, ...), custom_call_target="tpu_custom_call" | custom-call | tf_op jit(solution)/shard_map/pallas_call | solution.py:790
  37.2 0.6 %shard_map.123 = (f32[1,8]{1,0:T(1,128)}, bf16[1,8,512]{2,1,0:T(8,128)(2,1)}) custom-call(f32[1,8]{1,0:T(1,128)S(1)} %get-tuple-element.4.log_probs, bf16[1,8,512]{2,1,0:T(8,128)(2,1)S(1)} %get-tuple-element.5.normed), custom_call_target="tpu_custom_call" | custom-call | tf_op jit(solution)/shard_map/pallas_call | solution.py:858

commit v3 on v2

--- a/solution.py
+++ b/solution.py
@@ -117,7 +117,8 @@
 DEAD = -1e29
 TILE = 256
 SINGLE = 3
-TURNS = (3, 3, 5, 3, 2)
+FIRST = 4
+TURNS = (4, 3, 5, 3, 1)
 MESH = pl.DeviceIdType.MESH
 
 
@@ -184,14 +185,16 @@
     e_rs,
 ):
     role = lax.axis_index("role")
-    me = lax.axis_index("grp") * tp + lax.axis_index("tp")
+    grp = lax.axis_index("grp")
+    lane_of = lax.axis_index("tp")
+    me = grp * tp + lane_of
     core = me % 2
     chip = me // 2
     mate = me + 1 - 2 * core
     chips = n // 2
     near = chips // 2
     half = n // 2
-    side = chip // near
+    side = grp
     step = 1 - role
     rows = resid.shape[0]
     width = resid.shape[1]
@@ -219,15 +222,30 @@
             bit *= 2
         return out
 
-    def remote(src, dst, ss, rs, to_role, place):
+    steps_of = [lane_of]
+    bit = 1
+    while bit < tp:
+        change = bit - 2 * bit * (lane_of // bit % 2)
+        steps_of += [at + change for at in steps_of]
+        bit *= 2
+    grps = (grp, 1 - grp)
+    roles = (role, 1 - role)
+
+    def peer(i, other_role=0):
+        return roles[other_role], grps[i // tp], steps_of[i % tp]
+
+    def remote(src, dst, ss, rs, where):
         return pltpu.make_async_remote_copy(
             src_ref=src,
             dst_ref=dst,
             send_sem=ss,
             recv_sem=rs,
-            device_id=(to_role, place // tp, place % tp),
+            device_id=where,
             device_id_type=MESH,
         )
+
+    here = peer(0)
+    mate_at = peer(1)
 
     def landed(ref, sem):
         pltpu.make_async_copy(ref, ref, sem).wait()
@@ -255,15 +273,9 @@
     loads[0].start()
     barrier = pltpu.get_barrier_semaphore()
     for i in range(1, 2 * n):
-        other = (role * n + me + i) % (2 * n)
         pl.semaphore_signal(
-            barrier,
-            inc=1,
-            device_id=(other // n, other % n // tp, other % tp),
-            device_id_type=MESH,
+            barrier, inc=1, device_id=peer(i % n, i // n), device_id_type=MESH
         )
-    for copy in loads[1:-1]:
-        copy.start()
     first_row = pl.multiple_of(role * (vocab - kept), 8)
 
     def direct(i):
@@ -284,41 +296,35 @@
     def far_copy(i):
         return head_copy(relayed(i), far_head, i, chips + i)
 
-    @pl.loop(0, TURNS[0])
-    def _(i):
+    for copy in loads[1:-1]:
+        copy.start()
+    for i in range(FIRST):
         near_copy(i).start()
-
     loads[-1].start()
-
-    @pl.loop(TURNS[0], chips)
-    def _(i):
+    for i in range(FIRST, chips):
         near_copy(i).start()
-
-    @pl.loop(0, chips)
-    def _(i):
-        far_copy(i).start()
-
     pl.semaphore_wait(barrier, 2 * n - 1)
     loads[0].wait()
 
     own_slot = me % half
     for i in range(chips - 1, 0, -1):
-        to = 2 * flip(chip, i, chips) + side
-        remote(q_own, q_all.at[own_slot], q_ss.at[i], q_rs.at[own_slot], role, to).start()
+        _, to_grp, to_lane = peer(2 * i)
+        to = role, to_grp, to_lane - core + side
+        remote(q_own, q_all.at[own_slot], q_ss.at[i], q_rs.at[own_slot], to).start()
 
     @pl.when(core != side)
     def _():
-        remote(q_own, q_all.at[own_slot], q_ss.at[0], q_rs.at[own_slot], role, mate).start()
+        remote(q_own, q_all.at[own_slot], q_ss.at[0], q_rs.at[own_slot], mate_at).start()
 
     @pl.when(core == side)
     def _():
         q_all[own_slot] = q_own[...]
 
     key_swap = remote(
-        keys_in.at[:, :, mate_keys], keys.at[core], k_ss.at[0], k_rs.at[0], role, mate
+        keys_in.at[:, :, mate_keys], keys.at[core], k_ss.at[0], k_rs.at[0], mate_at
     )
     value_swap = remote(
-        values_in.at[:, :, mate_keys], values.at[core], k_ss.at[1], k_rs.at[1], role, mate
+        values_in.at[:, :, mate_keys], values.at[core], k_ss.at[1], k_rs.at[1], mate_at
     )
     key_swap.start()
     value_swap.start()
@@ -363,7 +369,7 @@
     lane = lax.broadcasted_iota(jnp.int32, (rows, HEAD_SIZE), 1)
 
     def wait_query(slot):
-        remote(q_own, q_all.at[slot], q_ss.at[0], q_rs.at[slot], role, me).wait_recv()
+        remote(q_own, q_all.at[slot], q_ss.at[0], q_rs.at[slot], here).wait_recv()
 
     for i in range(near):
         local = flip(chip % near, i, near)
@@ -380,10 +386,10 @@
                 wait_query(slot + 1)
 
             remote(
-                keys_in.at[:, :, mate_keys], keys.at[1 - core], k_ss.at[0], k_rs.at[0], role, me
+                keys_in.at[:, :, mate_keys], keys.at[1 - core], k_ss.at[0], k_rs.at[0], here
             ).wait_recv()
             remote(
-                values_in.at[:, :, mate_keys], values.at[1 - core], k_ss.at[1], k_rs.at[1], role, me
+                values_in.at[:, :, mate_keys], values.at[1 - core], k_ss.at[1], k_rs.at[1], here
             ).wait_recv()
         else:
             wait_query(slot)
@@ -425,8 +431,9 @@
             ).astype(bf16)
         for part in range(2):
             to = core * half + slot + part
+            where = role, core, steps_of[2 * i] - core + part
             copy = remote(
-                b_send.at[slot + part], b_recv.at[chip], b_ss.at[2 * i + part], b_rs, role, to
+                b_send.at[slot + part], b_recv.at[chip], b_ss.at[2 * i + part], b_rs, where
             )
             if i == 0:
 
@@ -441,6 +448,8 @@
             else:
                 copy.start()
 
+    for i in range(chips):
+        far_copy(i).start()
     for copy in loads[4:9]:
         copy.wait()
     own_query = q_own[...].astype(f32)
@@ -514,7 +523,9 @@
             c_send[base + j] = out[:, j * width : (j + 1) * width].astype(bf16)
         for j in range(block):
             to = base + j
-            copy = remote(c_send.at[to], c_recv.at[me], c_ss, c_rs, role, to)
+            _, to_grp, to_lane = peer(block * i)
+            where = role, to_grp, to_lane - me % block + j
+            copy = remote(c_send.at[to], c_recv.at[me], c_ss, c_rs, where)
             if i == 0:
 
                 @pl.when(to != me)
@@ -537,31 +548,27 @@
     mine = slot_of(role, me)
     x_all[mine] = (state * gain[...]).astype(bf16)
 
-    def x_copy(slot, rs, ss, to_role, to):
-        return remote(x_all.at[slot], x_all.at[slot], ss, rs, to_role, to)
+    def x_copy(slot, rs, ss, where):
+        return remote(x_all.at[slot], x_all.at[slot], ss, rs, where)
 
     for i in range(chips):
-        to = 2 * flip(chip, i, chips) + core
-        x_copy(mine, x_rs.at[mine], d_ss, 1 - role, to).start()
-        if i == 0:
-            to = mate
-        x_copy(mine, x_rs.at[mine], d_ss, role, to).start()
+        x_copy(mine, x_rs.at[mine], d_ss, peer(2 * i, 1)).start()
+        x_copy(mine, x_rs.at[mine], d_ss, peer(2 * i) if i else mate_at).start()
 
     diagonal = lax.broadcasted_iota(jnp.int32, (rows, HEAD_SIZE), 0)
     square = jnp.sum(state * state, axis=1, keepdims=True)
     s_send[...] = jnp.sum(jnp.where(diagonal == lane, square, 0.0), axis=0, keepdims=True)
     own_stat = role * n + me
     for i in range(n - 1, -1, -1):
-        to = flip(me, i, n)
-        remote(s_send, s_recv.at[own_stat], s_ss, s_rs, 1 - role, to).start()
+        remote(s_send, s_recv.at[own_stat], s_ss, s_rs, peer(i, 1)).start()
         if i:
-            remote(s_send, s_recv.at[own_stat], s_ss, s_rs, role, to).start()
+            remote(s_send, s_recv.at[own_stat], s_ss, s_rs, peer(i)).start()
     s_recv[own_stat] = s_send[...]
 
     turn(3)
 
     def wait_x(slot):
-        x_copy(slot, x_rs.at[slot], d_ss, role, me).wait_recv()
+        x_copy(slot, x_rs.at[slot], d_ss, here).wait_recv()
 
     def features(place):
         return jnp.concatenate(
@@ -595,7 +602,7 @@
 
     def take(slot):
         wait_x(slot)
-        x_copy(slot, x_rs.at[slot], f_ss, role, mate).start()
+        x_copy(slot, x_rs.at[slot], f_ss, mate_at).start()
 
     def wait_far(i):
         place = relayed(i)
@@ -693,32 +700,31 @@
         packed = jnp.where(lane == diagonal + 2 * rows, target[part], packed)
         e_send[t] = jnp.sum(packed, axis=0, keepdims=True)
     for i in range(n - 1, -1, -1):
-        to = flip(me, i, n)
-        remote(e_send.at[1 - role], e_recv.at[own_stat], e_ss, e_rs, 1 - role, to).start()
+        remote(e_send.at[1 - role], e_recv.at[own_stat], e_ss, e_rs, peer(i, 1)).start()
         if i:
-            remote(e_send.at[role], e_recv.at[own_stat], e_ss, e_rs, role, to).start()
+            remote(e_send.at[role], e_recv.at[own_stat], e_ss, e_rs, peer(i)).start()
     e_recv[own_stat] = e_send[role]
 
     n_send[...] = (state * own_inverse * gain[...]).astype(bf16)
-    n_copy = remote(n_send, n_recv, n_sems.at[0], n_sems.at[1], 1 - role, me)
+    n_copy = remote(n_send, n_recv, n_sems.at[0], n_sems.at[1], peer(0, 1))
     n_copy.start()
 
     n_copy.wait_recv()
     normed[0] = n_recv[...]
     n_copy.wait_send()
     for i in range(1, chips):
-        remote(q_own, q_all.at[own_slot], q_ss.at[i], q_rs.at[own_slot], role, me).wait_send()
+        remote(q_own, q_all.at[own_slot], q_ss.at[i], q_rs.at[own_slot], here).wait_send()
 
     @pl.when(core != side)
     def _():
-        remote(q_own, q_all.at[own_slot], q_ss.at[0], q_rs.at[own_slot], role, mate).wait_send()
+        remote(q_own, q_all.at[own_slot], q_ss.at[0], q_rs.at[own_slot], mate_at).wait_send()
 
     key_swap.wait_send()
     value_swap.wait_send()
     for i in range(near):
         for part in range(2):
             copy = remote(
-                b_send.at[0], b_recv.at[chip], b_ss.at[2 * i + part], b_rs, role, me
+                b_send.at[0], b_recv.at[chip], b_ss.at[2 * i + part], b_rs, here
             )
             if i == 0:
 
@@ -871,7 +877,7 @@
     width = queries.shape[2]
     group = QUERY_HEADS // KEY_VALUE_HEADS
     whole_heads = width % HEAD_SIZE == 0 and 2 * (width // HEAD_SIZE) == group
-    powers = n & (n - 1) == 0 and n >= 8 and tp % 2 == 0 and n // 2 == KEY_VALUE_HEADS
+    powers = n & (n - 1) == 0 and n >= 8 and tp % 2 == 0 and n // 2 == KEY_VALUE_HEADS == tp
     fits = lax.axis_size("role") == 2 and powers and lengths.shape[0] == 8
     if whole_heads and fits and head.shape[0] == n * width and head.shape[1] % 8 == 0:
         return fused(*args)

time: 38 us -> 37.5 us (0.987)
  Pallas kernels: 37.2 us -> 36.7 us
    pallas_call x1, Pallas kernels: 36.6 us -> 36.1 us  [fused(): pl.pallas_call(functools.partial(fused_kernel, n, tp), out_shape=(pltpu.V...]
where the time goes in v3:
time: 37.5 us; the launch traced here: 37.3 us
  Pallas kernels  36.7 us (98%)
  between operations  0.64 us (2%)
    pallas_call x1, Pallas kernels, fused(): pl.pallas_call(functools.partial(fused_kernel, n, tp), out_shape=(pltpu.V...  36.1 us

profile of v3, /device:TPU:0, one launch (start us, length us, event | category | flops | bytes accessed | tf_op | source)
XLA Modules:
  0.0 37.3 jit_solution(325496865972396973)
XLA Ops:
  0.6 36.1 %shard_map.122 = (f32[1,8]{1,0:T(1,128)S(1)}, bf16[1,8,512]{2,1,0:T(8,128)(2,1)S(1)}) custom-call(bf16[2,8,512]{2,1,0:T(8,128)(2,1)} %queries.1, bf16[2,8,1024]{2,1,0:T(8,128)(2,1)} %token_keys.1, bf16[2,8,1024]{2,1,0:T(8,128)(2,1)} %token_values.1, bf16[8,32,1024]{2,1,0:T(8,128)(2,1)} %keys_in.1, bf16[8,32,1024]{2,1,0:T(8,128)(2,1)} %values_in.1, ...), custom_call_target="tpu_custom_call" | custom-call | tf_op jit(solution)/shard_map/pallas_call | solution.py:796
  36.7 0.6 %shard_map.123 = (f32[1,8]{1,0:T(1,128)}, bf16[1,8,512]{2,1,0:T(8,128)(2,1)}) custom-call(f32[1,8]{1,0:T(1,128)S(1)} %get-tuple-element.4.log_probs, bf16[1,8,512]{2,1,0:T(8,128)(2,1)S(1)} %get-tuple-element.5.normed), custom_call_target="tpu_custom_call" | custom-call | tf_op jit(solution)/shard_map/pallas_call | solution.py:864
